TPU v7x, 32 devices: a whole 2x2x4 slice. The times are simulated.
32 devices in a mesh: section: 4 (over y, x), tok: 8 (over z, core).
Axes of the slice: x: 2, y: 2, z: 4, core: 2. Of those that a mesh axis runs over, the one named last changes fastest.
Arguments:
- activations: bfloat16 [8, 2048, 8192], P('section', 'tok'), may hold values from -12 to 12
- projection: bfloat16 [8192, 512], P('tok'), may hold values from -0.0625 to 0.0625
Outputs:
- sketch: float32 [8, 512, 512], P('section', None, 'tok')
- similarity: float32 [8, 2], P('section')
All inputs are finite; a program needn't handle non-finite values.
Results may differ from a plain program's by a relative error of at most 0.0003.
Values may be sent and summed in bfloat16 or wider, within the bound.
A program may use at most 64 MiB of HBM per device.

v0:
```python
import jax
import jax.numpy as jnp
from jax import lax
from jax.sharding import PartitionSpec as P


def shifted(block, axis, distance):
    devices = range(lax.axis_size(axis))
    route = [(i - distance, i) for i in devices if i - distance in devices]
    return lax.ppermute(block, axis, route)


def frobenius(first, second):
    return jnp.sum(first * second, axis=(-2, -1))


def local_products(local_sketch, prev_last, next_first, section_index, sections):
    before = jnp.where(section_index == 0, local_sketch[0], prev_last)
    beyond = jnp.where(section_index == sections - 1, local_sketch[-1], next_first)
    squares = frobenius(local_sketch, local_sketch)
    chained = frobenius(local_sketch[:-1], local_sketch[1:])
    edges = jnp.stack(
        [
            frobenius(before, local_sketch[0]),
            frobenius(local_sketch[-1], beyond),
            frobenius(before, before),
            frobenius(beyond, beyond),
        ]
    )
    return jnp.concatenate([squares, chained, edges])


def finish(products, layers):
    squares = products[:layers]
    chained = products[layers : 2 * layers - 1]
    edges = products[2 * layers - 1 :]
    ext_squares = jnp.concatenate([edges[2:3], squares, edges[3:4]])
    ext_chained = jnp.concatenate([edges[0:1], chained, edges[1:2]])
    ratios = ext_chained / jnp.sqrt(ext_squares[:-1] * ext_squares[1:])
    return jnp.stack([ratios[:-1], ratios[1:]], axis=1)


def local(activations, projection):
    layers, tok_rows, model_width = activations.shape
    sketch_width = projection.shape[1]
    groups = lax.axis_size("tok")
    total_tokens = tok_rows * groups
    flat_acts = activations.reshape(layers * tok_rows, model_width)
    projected = jnp.dot(
        flat_acts,
        lax.all_gather(projection, "tok", axis=0, tiled=True),
        preferred_element_type=jnp.float32,
    )
    projected = projected.reshape(layers, tok_rows, sketch_width)
    raw_gram = jnp.einsum("ltr,lts->lrs", projected, projected, precision=lax.Precision.HIGHEST)
    local_sums = jnp.sum(projected, axis=1)
    tok_index = lax.axis_index("tok")
    section_index = lax.axis_index("section")
    sections = lax.axis_size("section")
    columns_dev = sketch_width // groups
    shares = lax.psum_scatter(raw_gram, "tok", scatter_dimension=2, tiled=True)
    totals = lax.psum(local_sums, "tok")
    local_totals = lax.dynamic_slice_in_dim(totals, tok_index * columns_dev, columns_dev, 1)
    local_sketch = shares - totals[:, :, None] * local_totals[:, None, :] / total_tokens
    next_first = shifted(local_sketch[0].astype(jnp.bfloat16), "section", -1).astype(jnp.float32)
    prev_last = shifted(local_sketch[layers - 1].astype(jnp.bfloat16), "section", 1).astype(
        jnp.float32
    )
    partial_products = local_products(local_sketch, prev_last, next_first, section_index, sections)
    products = lax.psum(partial_products, "tok")
    return (local_sketch, finish(products, layers))


def solution(mesh):
    return jax.shard_map(
        local,
        mesh=mesh,
        in_specs=(P("section", "tok", None), P("tok", None)),
        out_specs=(P("section", None, "tok"), P("section", None)),
        check_vma=False,
    )
```

profile of v0, /device:TPU:0, one launch (start us, length us, event | category | flops | bytes accessed | tf_op | source)
XLA Modules:
  0.0 179.9 jit_solution(8922740263490484385)
XLA Ops:
  7.2 0.0 all-gather.2.cloned.1.call-start
  7.2 0.7 all-gather.2.cloned.1.call-update
  7.9 0.0 reduce-scatter.2.cloned.1.call-start
  7.9 86.4 %all-gather.2.cloned.1.call-done = bf16[8192,512]{1,0:T(8,128)(2,1)} async-done(((bf16[1024,512]{1,0:T(8,128)(2,1)}), bf16[8192,512]{1,0:T(8,128)(2,1)}) %all-gather.2.cloned.1.call-update) | async-done | bytes 8388624 | tf_op jit(solution)/shard_map/all_gather | solution.py:51
  94.4 9.5 %fusion.6 = (f32[2,512]{1,0:T(2,128)S(1)}, f32[2,256,512]{2,1,0:T(8,128)S(1)}) fusion(bf16[2,256,8192]{2,1,0:T(8,128)(2,1)} %param.2, bf16[8192,512]{1,0:T(8,128)(2,1)} %all-gather.2.cloned.1.call-done), kind=kOutput, calls=%fused_computation.23 | convolution fusion | flops 4295228416 | bytes 17829888 | tf_op jit(solution)/shard_map/dot_general | solution.py:49
  103.9 3.3 %fusion.7 = f32[2,512,512]{1,2,0:T(8,128)} fusion(f32[2,256,512]{2,1,0:T(8,128)S(1)} %get-tuple-element.22), kind=kOutput, calls=%fused_computation.24 | convolution fusion | flops 1610612736 | bytes 3145728 | tf_op jit(solution)/shard_map/ltr,lts->lrs/dot_general | solution.py:55
  107.2 0.0 reduce-scatter.2.cloned.1.call-update
  107.2 14.4 %psum.14 = f32[2,512]{1,0:T(2,128)S(1)} all-reduce(f32[2,512]{1,0:T(2,128)S(1)} %get-tuple-element.21), channel_id=1, replica_groups=mesh['section'=4,'tok'=8] {'tok'}, use_global_device_ids=true, to_apply=%region_2.0 | all-reduce | flops 1024 | bytes 8192 | tf_op jit(solution)/shard_map/psum | solution.py:62
  121.6 0.1 constant_dynamic-slice_fusion
  121.7 20.2 %reduce-scatter.2.cloned.1.call-done = f32[2,512,64]{1,2,0:T(8,128)} async-done(((f32[2,512,512]{1,2,0:T(8,128)}), f32[2,512,64]{1,2,0:T(8,128)}) %reduce-scatter.2.cloned.1.call-update) | async-done | bytes 262160 | tf_op jit(solution)/shard_map/reduce_scatter | solution.py:61
  141.9 1.2 multiply_reduce_fusion
  143.1 0.0 copy-start
  143.1 1.3 collective-permute-start.1
  144.4 4.5 %collective-permute-start = (bf16[512,64]{0,1:T(8,128)(2,1)S(1)}, bf16[512,64]{0,1:T(8,128)(2,1)S(1)}, u32[]{:S(2)}, u32[]{:S(2)}) collective-permute-start(bf16[512,64]{0,1:T(8,128)(2,1)S(1)} %get-tuple-element.12), channel_id=1, source_target_pairs={{0,8},{8,16},{16,24},{1,9},{9,17},{17,25},{2,10},{10,18},{18,26},{... | collective-permute-start | bytes 196616 | tf_op jit(solution)/shard_map/ppermute | solution.py:10
  149.0 0.6 multiply_reduce_fusion.3
  149.6 0.1 collective-permute-done.1
  149.7 1.1 collective-permute-done
  150.8 0.7 multiply_reduce_fusion.1
  151.6 3.2 %concatenate.13 = f32[7]{0:T(128)S(1)} concatenate(f32[2]{0:T(128)S(1)} %get-tuple-element.10, f32[1]{0:T(128)} %bitcast.1, f32[1]{0:T(128)} %bitcast.4, f32[1]{0:T(128)} %bitcast.5, f32[1]{0:T(128)} %bitcast.6, f32[1]{0:T(128)} %bitcast.7), dimensions={0} | concatenate | bytes 56 | tf_op jit(solution)/shard_map/concatenate | solution.py:30
  154.8 13.6 %psum.15 = f32[7]{0:T(128)S(1)} all-reduce(f32[7]{0:T(128)S(1)} %concatenate.13), channel_id=1, replica_groups=mesh['section'=4,'tok'=8] {'tok'}, use_global_device_ids=true, to_apply=%region_9.10 | all-reduce | flops 7 | bytes 56 | tf_op jit(solution)/shard_map/psum | solution.py:70
  168.4 0.7 fusion.5
  169.1 3.2 %maximum_multiply_fusion = f32[3]{0:T(128)S(1)} fusion(f32[1]{0:T(128)} %get-tuple-element.18, f32[1]{0:T(128)} %get-tuple-element.19, f32[1]{0:T(128)} %get-tuple-element.20, f32[2]{0:T(128)S(1)} %bitcast.38, f32[1]{0:T(128)} %get-tuple-element.17, f32[1]{0:T(128)} %get-tuple-element.16), kind=kLoop, calls=%fused_computation.16 | loop fusion | flops 18 | bytes 40 | tf_op jit(solution)/shard_map/div | solution.py:39
  172.3 0.1 slice_bitcast_fusion.1
  172.4 0.7 copy.5
  173.0 0.0 copy-done
  (2 shorter events, 0.0 us)
Async XLA Ops:
  7.2 87.2 %all-gather.2.cloned.1.call-start = ((), (), s32[]{:S(2)}) async-start(), calls=%async_computation.1 | async-start | bytes 9437184 | tf_op jit(solution)/shard_map/all_gather | solution.py:51
  7.9 134.0 %reduce-scatter.2.cloned.1.call-start = ((), (), s32[]{:S(2)}) async-start(), calls=%async_computation.2 | async-start | bytes 2359296 | tf_op jit(solution)/shard_map/reduce_scatter | solution.py:61
  143.1 30.0 %copy-start = (f32[2,512,64]{1,2,0:T(8,128)}, f32[2,512,64]{1,2,0:T(8,128)S(1)}, u32[]{:S(2)}) copy-start(f32[2,512,64]{1,2,0:T(8,128)S(1)} %get-tuple-element.11) | copy-start | bytes 786436
  143.1 6.6 %collective-permute-start.1 = (bf16[512,64]{0,1:T(8,128)(2,1)S(1)}, bf16[512,64]{0,1:T(8,128)(2,1)S(1)}, u32[]{:S(2)}, u32[]{:S(2)}) collective-permute-start(bf16[512,64]{0,1:T(8,128)(2,1)S(1)} %get-tuple-element.13), channel_id=1, source_target_pairs={{8,0},{16,8},{24,16},{9,1},{17,9},{25,17},{10,2},{18,10},{26,18},{... | collective-permute-start | bytes 196616 | tf_op jit(solution)/shard_map/ppermute | solution.py:10
  144.4 6.4 %collective-permute-start = (bf16[512,64]{0,1:T(8,128)(2,1)S(1)}, bf16[512,64]{0,1:T(8,128)(2,1)S(1)}, u32[]{:S(2)}, u32[]{:S(2)}) collective-permute-start(bf16[512,64]{0,1:T(8,128)(2,1)S(1)} %get-tuple-element.12), channel_id=1, source_target_pairs={{0,8},{8,16},{16,24},{1,9},{9,17},{17,25},{2,10},{10,18},{18,26},{... | collective-permute-start | bytes 196616 | tf_op jit(solution)/shard_map/ppermute | solution.py:10
Sparse Core Ops, SparseCore 0:
  9.6 84.7 all-gather.1
  107.3 34.5 reduce-scatter.1
where the time goes:
time: 181 us; the launch traced here: 180 us
  waiting for transfers between devices  109 us (60%)
  blocking collectives  28 us (15%)
  between operations  14.1 us (8%)
  matrix products  12.8 us (7%)
  starting transfers between devices  5.92 us (3%)
  other arithmetic  5.78 us (3%)
  local copies, waits for them, and re-layouts  4.73 us (3%)
    all_gather x1, waiting for transfers between devices, local(): lax.all_gather(projection, 'tok', axis=0, tiled=True)  86.4 us
    reduce_scatter x1, waiting for transfers between devices, local(): shares = lax.psum_scatter(raw_gram, 'tok', scatter_dimension=2, tiled=True)  20.2 us
    psum x1, blocking collectives, local(): totals = lax.psum(local_sums, 'tok')  14.4 us
    psum x1, blocking collectives, local(): products = lax.psum(partial_products, 'tok')  13.6 us
    dot_general x1, matrix products, local(): jnp.dot(flat_acts, lax.all_gather(projection, 'tok', axis=0, tiled=True),...  9.49 us
    ppermute x2, starting transfers between devices, shifted(): return lax.ppermute(block, axis, route)  5.84 us
  transfers between devices with their start and end apart: 4, of which 4 were waited for; matrix products, arithmetic and copies ran while one was open for 0% of the time, Pallas kernels for 0%

commit v1 on v0

v1 whole, which is shorter than its diff:
```python
import functools

import jax
import jax.numpy as jnp
from jax import lax
from jax.experimental import pallas as pl
from jax.experimental.pallas import tpu as pltpu
from jax.sharding import PartitionSpec as P

F32, BF16 = jnp.float32, jnp.bfloat16


def flip(index, mask, size):
    result, bit = 0, 1
    while bit < size:
        digit = (index // bit) % 2
        result = result + bit * ((1 - digit) if mask & bit else digit)
        bit *= 2
    return result


def snake(place, sections):
    half = sections // 2
    return jnp.where(place < half, place, 3 * half - 1 - place)


def kernel(
    sections, groups, layers, acts_hbm, proj_hbm, sketch_ref, sim_ref,
    acts, proj, total, left_op, right_op, gram, pair_in, line_in, mean_out, means, corr,
    edge_out, edge_in, prod_out, prods,
    acts_sem, own_sem, d2d_own, line_s, line_r, ring_s, ring_r, d2d_s, d2d_r,
    mean_s, mean_r, pair_s, pair_r, gl_s, gl_r, edge_s, edge_r, prod_s, prod_r,
):
    section = lax.axis_index("section")
    tok = lax.axis_index("tok")
    chips = groups // 2
    chip, core = tok // 2, tok % 2
    partner = chip * 2 + 1 - core
    rows = acts.shape[1]
    tok_rows = rows // layers
    depth = proj.shape[1]
    width = proj.shape[2]
    slab = width // groups
    half_ring = sections // 2
    piece = depth // sections
    part = piece // 2
    place = snake(section, sections)
    to_right = snake((place + 1) % sections, sections)
    to_left = snake((place + sections - 1) % sections, sections)

    own_copy = pltpu.make_async_copy(proj_hbm, proj.at[tok], own_sem)
    own_copy.start()
    order = [tok, partner]
    for k in range(1, chips):
        other = flip(chip, k, chips)
        order += [other * 2 + core, other * 2 + 1 - core]
    loads = []
    for n, t in enumerate(order):
        start = pl.multiple_of(t * depth, depth)
        loads.append(
            pltpu.make_async_copy(acts_hbm.at[:, pl.ds(start, depth)], acts.at[n], acts_sem.at[n])
        )
        loads[-1].start()

    barrier = pltpu.get_barrier_semaphore()
    for d in range(1, groups):
        pl.semaphore_signal(
            barrier, inc=1, device_id={"tok": (tok + d) % groups}, device_id_type=pl.DeviceIdType.MESH
        )
    for d in range(1, sections):
        pl.semaphore_signal(
            barrier, inc=1, device_id={"section": (section + d) % sections},
            device_id_type=pl.DeviceIdType.MESH,
        )
    pl.semaphore_wait(barrier, groups - 1 + sections - 1)

    pending = []

    def send(src, dst, send_sem, recv_sem, **where):
        copy = pltpu.make_async_remote_copy(
            src_ref=src, dst_ref=dst, send_sem=send_sem, recv_sem=recv_sem,
            device_id=where, device_id_type=pl.DeviceIdType.MESH,
        )
        copy.start()
        pending.append(copy)
        return copy

    def halves(t, at, h):
        start = pl.multiple_of((at % sections) * piece + h * part, part)
        return proj.at[t, pl.ds(start, part)]

    own_copy.wait()
    line = {}
    for k in range(1, chips):
        for h in range(2):
            ref = halves(tok, place, h)
            line[k, h] = send(
                ref, ref, line_s.at[k - 1, h], line_r.at[k - 1, h], tok=flip(chip, k, chips) * 2 + core
            )
    partner_slab = send(proj.at[tok], proj.at[tok], d2d_own.at[0], d2d_own.at[1], tok=partner)

    def multiply(n, first=False):
        loads[n].wait()
        product = jnp.dot(acts[n], proj[order[n]], preferred_element_type=F32)
        if first:
            total[...] = product
        else:
            total[...] += product

    multiply(0, True)
    partner_slab.wait_recv()
    multiply(1)

    shared = {k: [] for k in range(1, chips)}
    ring = {}

    def share(k, ref):
        n = len(shared[k])
        shared[k].append(send(ref, ref, d2d_s.at[k - 1, n], d2d_r.at[k - 1, n], tok=partner))

    def pass_on(k, j, way, h, ref):
        ring[k, j, way, h] = send(
            ref, ref, ring_s.at[k - 1, j - 1, way, h], ring_r.at[k - 1, j - 1, way, h],
            section=(to_right if way == 0 else to_left),
        )

    events = []
    for k in range(1, chips):
        events.append((2 * k, k, 0))
        for j in range(1, half_ring + 1):
            events.append((3 * k + j - 1, k, j))
    for _, k, j in sorted(events):
        t = order[2 * k]
        if j == 0:
            for h in range(2):
                line[k, h].wait_recv()
                ref = halves(t, place, h)
                for way in range(2):
                    if half_ring > 1 or way == h:
                        pass_on(k, 1, way, h, ref)
                share(k, ref)
        else:
            for h in range(2):
                for way in range(2):
                    if j == half_ring and way != h:
                        continue
                    ring[k, j, way, h].wait_recv()
                    at = place + sections - j if way == 0 else place + j
                    ref = halves(t, at, h)
                    if j < half_ring and (j + 1 < half_ring or way == h):
                        pass_on(k, j + 1, way, h, ref)
                    share(k, ref)
            if j == half_ring:
                multiply(2 * k)
                for copy in shared[k]:
                    copy.wait_recv()
                multiply(2 * k + 1)

    mean_out[...] = jnp.zeros_like(mean_out)
    for l in range(layers):
        block = total[l * tok_rows : (l + 1) * tok_rows]
        mean = jnp.sum(block, axis=0, keepdims=True) / tok_rows
        mean_out[l : l + 1] = mean
        block = block - mean
        high = block.astype(BF16)
        low = (block - high.astype(F32)).astype(BF16)
        left_op[l, :tok_rows] = high
        left_op[l, tok_rows : 2 * tok_rows] = high
        left_op[l, 2 * tok_rows :] = low
        right_op[l, :tok_rows] = high
        right_op[l, tok_rows : 2 * tok_rows] = low
        right_op[l, 2 * tok_rows :] = high
    mean_copies = []
    for k in range(1, groups):
        mean_copies.append(
            send(mean_out, means.at[k - 1], mean_s.at[k - 1], mean_r.at[k - 1], tok=flip(tok, k, groups))
        )

    pair = {}
    for l in range(layers):
        product = lax.dot_general(
            left_op[l], right_op[l], (((0,), (0,)), ((), ())), preferred_element_type=F32
        )
        for t in range(groups):
            gram[t, l] = product[t * slab : (t + 1) * slab]
        for k in list(range(1, chips)) + [0]:
            other = flip(chip, k, chips)
            pair[k, l] = send(
                gram.at[other * 2 + 1 - core, l], pair_in.at[k, l], pair_s.at[k, l], pair_r.at[k, l],
                tok=partner,
            )
    far = {}
    for l in range(layers):
        for k in list(range(1, chips)) + [0]:
            other = flip(chip, k, chips) * 2 + core
            pair[k, l].wait_recv()
            gram[other, l] = gram[other, l] + pair_in[k, l]
            if k:
                far[k, l] = send(
                    gram.at[other, l], line_in.at[k - 1, l], gl_s.at[k - 1, l], gl_r.at[k - 1, l],
                    tok=other,
                )

    for copy in mean_copies:
        copy.wait_recv()
    overall = mean_out[...]
    for k in range(1, groups):
        overall = overall + means[k - 1]
    overall = overall / groups
    for l in range(layers):
        shifts = [mean_out[l : l + 1] - overall[l : l + 1]]
        for k in range(1, groups):
            shifts.append(means[k - 1, l : l + 1] - overall[l : l + 1])
        shifts = jnp.concatenate(shifts, axis=0)
        outer = lax.dot_general(
            shifts, shifts * tok_rows, (((0,), (0,)), ((), ())),
            precision=lax.Precision.HIGHEST, preferred_element_type=F32,
        )
        for t in range(groups):
            corr[t, l] = outer[t * slab : (t + 1) * slab]

    edge = {}
    for l in range(layers):
        result = gram[tok, l] + corr[tok, l]
        for k in range(1, chips):
            far[k, l].wait_recv()
            result = result + line_in[k - 1, l]
        sketch_ref[l] = result
        if l == 0:
            edge_out[0] = result.astype(BF16)
            edge[0] = send(
                edge_out.at[0], edge_in.at[0], edge_s.at[0], edge_r.at[0],
                section=(section + sections - 1) % sections,
            )
        if l == layers - 1:
            edge_out[1] = result.astype(BF16)
            edge[1] = send(
                edge_out.at[1], edge_in.at[1], edge_s.at[1], edge_r.at[1],
                section=(section + 1) % sections,
            )

    def inner(first, second):
        columns = jnp.sum(first * second, axis=0, keepdims=True)
        lanes = columns[:, :128]
        for start in range(128, width, 128):
            lanes = lanes + columns[:, start : start + 128]
        return lanes

    prod_out[...] = jnp.zeros_like(prod_out)
    own = [sketch_ref[l] for l in range(layers)]
    for l in range(layers):
        prod_out[l : l + 1] = inner(own[l], own[l])
        if l:
            prod_out[layers + l - 1 : layers + l] = inner(own[l - 1], own[l])
    base = 2 * layers - 1
    edge[0].wait_recv()
    beyond = jnp.where(section == sections - 1, own[-1], edge_in[0].astype(F32))
    prod_out[base : base + 1] = inner(own[-1], beyond)
    prod_out[base + 1 : base + 2] = inner(beyond, beyond)
    edge[1].wait_recv()
    before = jnp.where(section == 0, own[0], edge_in[1].astype(F32))
    prod_out[base + 2 : base + 3] = inner(own[0], before)
    prod_out[base + 3 : base + 4] = inner(before, before)
    prod_copies = []
    for k in range(1, groups):
        prod_copies.append(
            send(prod_out, prods.at[k - 1], prod_s.at[k - 1], prod_r.at[k - 1], tok=flip(tok, k, groups))
        )
    products = prod_out[...]
    for k in range(1, groups):
        prod_copies[k - 1].wait_recv()
        products = products + prods[k - 1]
    products = jnp.broadcast_to(jnp.sum(products, axis=1, keepdims=True), products.shape)

    def item(i):
        return products[i : i + 1]

    squares = [item(base + 3)] + [item(l) for l in range(layers)] + [item(base + 1)]
    chained = [item(base + 2)] + [item(layers + l) for l in range(layers - 1)] + [item(base)]
    ratios = [chained[i] / jnp.sqrt(squares[i] * squares[i + 1]) for i in range(layers + 1)]
    sim_ref[...] = jnp.zeros_like(sim_ref)
    lane = lax.broadcasted_iota(jnp.int32, (1, 128), 1)
    for l in range(layers):
        sim_ref[l : l + 1] = jnp.where(lane == 0, ratios[l], ratios[l + 1])

    for copy in pending:
        copy.wait_send()


def local(sections, groups, activations, projection):
    layers, tok_rows, model_width = activations.shape
    depth, width = projection.shape
    rows = layers * tok_rows
    chips, slab = groups // 2, width // groups
    tall = -(-(2 * layers + 3) // 8) * 8
    dma = pltpu.SemaphoreType.DMA
    sketch, sim = pl.pallas_call(
        functools.partial(kernel, sections, groups, layers),
        out_shape=(
            jax.ShapeDtypeStruct((layers, slab, width), F32),
            jax.ShapeDtypeStruct((tall, 128), F32),
        ),
        in_specs=[pl.BlockSpec(memory_space=pl.ANY)] * 2,
        out_specs=(pl.BlockSpec(memory_space=pltpu.VMEM),) * 2,
        scratch_shapes=[
            pltpu.VMEM((groups, rows, depth), BF16),
            pltpu.VMEM((groups, depth, width), BF16),
            pltpu.VMEM((rows, width), F32),
            pltpu.VMEM((layers, 3 * tok_rows, width), BF16),
            pltpu.VMEM((layers, 3 * tok_rows, width), BF16),
            pltpu.VMEM((groups, layers, slab, width), F32),
            pltpu.VMEM((chips, layers, slab, width), F32),
            pltpu.VMEM((chips - 1, layers, slab, width), F32),
            pltpu.VMEM((tall, width), F32),
            pltpu.VMEM((groups - 1, tall, width), F32),
            pltpu.VMEM((groups, layers, slab, width), F32),
            pltpu.VMEM((2, slab, width), BF16),
            pltpu.VMEM((2, slab, width), BF16),
            pltpu.VMEM((tall, 128), F32),
            pltpu.VMEM((groups - 1, tall, 128), F32),
            dma((groups,)), dma(()), dma((2,)),
            dma((chips - 1, 2)), dma((chips - 1, 2)),
            dma((chips - 1, sections // 2, 2, 2)), dma((chips - 1, sections // 2, 2, 2)),
            dma((chips - 1, 2 * sections)), dma((chips - 1, 2 * sections)),
            dma((groups - 1,)), dma((groups - 1,)),
            dma((chips, layers)), dma((chips, layers)),
            dma((chips - 1, layers)), dma((chips - 1, layers)),
            dma((2,)), dma((2,)),
            dma((groups - 1,)), dma((groups - 1,)),
        ],
        compiler_params=pltpu.CompilerParams(
            collective_id=0, has_side_effects=True, vmem_limit_bytes=60 * 1024 * 1024
        ),
    )(activations.reshape(rows, model_width), projection)
    return jnp.swapaxes(sketch, 1, 2), sim[:layers, :2]


def solution(mesh):
    return jax.shard_map(
        functools.partial(local, mesh.shape["section"], mesh.shape["tok"]),
        mesh=mesh,
        in_specs=(P("section", "tok", None), P("tok", None)),
        out_specs=(P("section", None, "tok"), P("section", None)),
        check_vma=False,
    )
```

time: 181 us -> 89.8 us (0.50)
  waiting for transfers between devices: 109 us -> 0 us
  Pallas kernels: 0 us -> 86.1 us
  blocking collectives: 28 us -> 0 us
  between operations: 14.1 us -> 0.64 us
  matrix products: 12.8 us -> 0 us
  starting transfers between devices: 5.92 us -> 0 us
  other arithmetic: 5.78 us -> 0 us
  local copies, waits for them, and re-layouts: 4.73 us -> 2.92 us
    all_gather x1 -> x0, waiting for transfers between devices: 86.4 us -> none  [local(): lax.all_gather(projection, 'tok', axis=0, tiled=True)]
    pallas_call x0 -> x1, Pallas kernels: none -> 86.1 us  [local(): pl.pallas_call(functools.partial(kernel, sections, groups, layers), out_s...]
    psum x2 -> x0, blocking collectives: 28 us -> none  [the longest x1 14.4 us: local(): totals = lax.psum(local_sums, 'tok')]
    reduce_scatter x1 -> x0, waiting for transfers between devices: 20.2 us -> none  [local(): shares = lax.psum_scatter(raw_gram, 'tok', scatter_dimension=2, tiled=True)]
    dot_general x2 -> x0, matrix products: 12.8 us -> none  [the longest x1 9.49 us: local(): jnp.dot(flat_acts, lax.all_gather(projection, 'tok', axis=0, tiled=True),...]
    ppermute x2 -> x0, starting transfers between devices: 5.84 us -> none  [shifted(): return lax.ppermute(block, axis, route)]
    concatenate x1 -> x0, local copies, waits for them, and re-layouts: 3.24 us -> none  [local_products(): return jnp.concatenate([squares, chained, edges])]
    div x1 -> x0, other arithmetic: 3.23 us -> none  [finish(): ratios = ext_chained / jnp.sqrt(ext_squares[:-1] * ext_squares[1:])]
  transfers between devices with their start and end apart: 4 -> 0, of which waited for: 4 -> 0; matrix products, arithmetic and copies ran while one was open for 0% -> 0% of each run, Pallas kernels for 0% -> 0%
where the time goes in v1:
time: 89.8 us; the launch traced here: 89.6 us
  Pallas kernels  86.1 us (96%)
  local copies, waits for them, and re-layouts  2.92 us (3%)
    pallas_call x1, Pallas kernels, local(): pl.pallas_call(functools.partial(kernel, sections, groups, layers), out_s...  86.1 us

profile of v1, /device:TPU:0, one launch (start us, length us, event | category | flops | bytes accessed | tf_op | source)
XLA Modules:
  0.0 89.6 jit_solution(15678425952100460012)
XLA Ops:
  0.6 86.1 %shard_map.41 = (f32[2,64,512]{2,1,0:T(8,128)}, f32[8,128]{1,0:T(8,128)}) custom-call(bf16[512,8192]{1,0:T(8,128)(2,1)} %bitcast.2, bf16[1024,512]{1,0:T(8,128)(2,1)} %proj_hbm.1), custom_call_target="tpu_custom_call" | custom-call | tf_op jit(solution)/shard_map/pallas_call | solution.py:297
  86.7 1.2 %slice.3 = f32[2,2]{1,0:T(2,128)} slice(f32[8,128]{1,0:T(8,128)} %get-tuple-element.5), slice={[0:2], [0:2]} | slice | bytes 32 | tf_op jit(solution)/shard_map/slice | solution.py:335
  88.0 1.7 %copy.5 = f32[2,512,64]{1,2,0:T(8,128)} copy(f32[2,512,64]{1,2,0:T(8,128)} %bitcast.3) | data formatting | bytes 524288

commit v2 on v1

--- a/solution.py
+++ b/solution.py
@@ -19,6 +19,14 @@
     return result
 
 
+def nearest(chip, n, chips):
+    short = jnp.minimum(chip, chips - 1 - chip)
+    paired = n <= 2 * short
+    distance = jnp.where(paired, (n + 1) // 2, n - short)
+    lower = jnp.where(paired, n % 2 == 1, chip >= chips // 2)
+    return jnp.where(lower, chip - distance, chip + distance)
+
+
 def snake(place, sections):
     half = sections // 2
     return jnp.where(place < half, place, 3 * half - 1 - place)
@@ -27,9 +35,9 @@
 def kernel(
     sections, groups, layers, acts_hbm, proj_hbm, sketch_ref, sim_ref,
     acts, proj, total, left_op, right_op, gram, pair_in, line_in, mean_out, means, corr,
-    edge_out, edge_in, prod_out, prods,
+    edge_out, edge_in, prod_out, prods, prev_prods,
     acts_sem, own_sem, d2d_own, line_s, line_r, ring_s, ring_r, d2d_s, d2d_r,
-    mean_s, mean_r, pair_s, pair_r, gl_s, gl_r, edge_s, edge_r, prod_s, prod_r,
+    mean_s, mean_r, pair_s, pair_r, gl_s, gl_r, edge_s, edge_r, prod_s, prod_r, prev_s, prev_r,
 ):
     section = lax.axis_index("section")
     tok = lax.axis_index("tok")
@@ -52,7 +60,7 @@
     own_copy.start()
     order = [tok, partner]
     for k in range(1, chips):
-        other = flip(chip, k, chips)
+        other = nearest(chip, k, chips)
         order += [other * 2 + core, other * 2 + 1 - core]
     loads = []
     for n, t in enumerate(order):
@@ -72,7 +80,15 @@
             barrier, inc=1, device_id={"section": (section + d) % sections},
             device_id_type=pl.DeviceIdType.MESH,
         )
-    pl.semaphore_wait(barrier, groups - 1 + sections - 1)
+    beside = sorted({1, sections - 1})
+    for away in beside:
+        for d in range(1, groups):
+            pl.semaphore_signal(
+                barrier, inc=1,
+                device_id={"section": (section + away) % sections, "tok": (tok + d) % groups},
+                device_id_type=pl.DeviceIdType.MESH,
+            )
+    pl.semaphore_wait(barrier, (groups - 1) * (1 + len(beside)) + sections - 1)
 
     pending = []
 
@@ -90,13 +106,27 @@
         return proj.at[t, pl.ds(start, part)]
 
     own_copy.wait()
-    line = {}
-    for k in range(1, chips):
-        for h in range(2):
-            ref = halves(tok, place, h)
-            line[k, h] = send(
-                ref, ref, line_s.at[k - 1, h], line_r.at[k - 1, h], tok=flip(chip, k, chips) * 2 + core
-            )
+
+    def line_copy(source, h, step):
+        ref = halves(source * 2 + core, place, h)
+        return pltpu.make_async_remote_copy(
+            src_ref=ref, dst_ref=ref,
+            send_sem=line_s.at[source, h, (step + 1) // 2], recv_sem=line_r.at[source, h],
+            device_id={"tok": (chip + step + chips) % chips * 2 + core},
+            device_id_type=pl.DeviceIdType.MESH,
+        )
+
+    def along(source, h, action):
+        for step in (-1, 1):
+            inside = chip + step <= chips - 1 if step == 1 else chip + step >= 0
+            away = source <= chip if step == 1 else source >= chip
+
+            @pl.when(jnp.logical_and(inside, away))
+            def _():
+                action(line_copy(source, h, step))
+
+    for h in range(2):
+        along(chip, h, lambda copy: copy.start())
     partner_slab = send(proj.at[tok], proj.at[tok], d2d_own.at[0], d2d_own.at[1], tok=partner)
 
     def multiply(n, first=False):
@@ -126,20 +156,23 @@
 
     events = []
     for k in range(1, chips):
-        events.append((2 * k, k, 0))
+        events.append((0.75 * k + 0.2, k, 0))
         for j in range(1, half_ring + 1):
-            events.append((3 * k + j - 1, k, j))
+            events.append((1.5 * k + 1.4 * j - 1.1, k, j))
+        events.append((1.5 * k + 1.4 * half_ring - 0.9, k, half_ring + 1))
     for _, k, j in sorted(events):
         t = order[2 * k]
         if j == 0:
             for h in range(2):
-                line[k, h].wait_recv()
+                source = t // 2
+                line_copy(source, h, 1).wait_recv()
                 ref = halves(t, place, h)
+                along(source, h, lambda copy: copy.start())
                 for way in range(2):
                     if half_ring > 1 or way == h:
                         pass_on(k, 1, way, h, ref)
                 share(k, ref)
-        else:
+        elif j <= half_ring:
             for h in range(2):
                 for way in range(2):
                     if j == half_ring and way != h:
@@ -150,11 +183,11 @@
                     if j < half_ring and (j + 1 < half_ring or way == h):
                         pass_on(k, j + 1, way, h, ref)
                     share(k, ref)
-            if j == half_ring:
-                multiply(2 * k)
-                for copy in shared[k]:
-                    copy.wait_recv()
-                multiply(2 * k + 1)
+        else:
+            multiply(2 * k)
+            for copy in shared[k]:
+                copy.wait_recv()
+            multiply(2 * k + 1)
 
     mean_out[...] = jnp.zeros_like(mean_out)
     for l in range(layers):
@@ -176,67 +209,123 @@
             send(mean_out, means.at[k - 1], mean_s.at[k - 1], mean_r.at[k - 1], tok=flip(tok, k, groups))
         )
 
+    low_side = chip < chips // 2
+    rank = jnp.where(low_side, chip, chips - 1 - chip)
+
+    def mirror(d):
+        return jnp.where(low_side, d, chips - 1 - d)
+
     pair = {}
+    outward = [chips - 1 - d for d in range(chips)]
     for l in range(layers):
         product = lax.dot_general(
             left_op[l], right_op[l], (((0,), (0,)), ((), ())), preferred_element_type=F32
         )
         for t in range(groups):
             gram[t, l] = product[t * slab : (t + 1) * slab]
-        for k in list(range(1, chips)) + [0]:
-            other = flip(chip, k, chips)
-            pair[k, l] = send(
-                gram.at[other * 2 + 1 - core, l], pair_in.at[k, l], pair_s.at[k, l], pair_r.at[k, l],
+        for d in outward:
+            pair[d, l] = send(
+                gram.at[mirror(d) * 2 + 1 - core, l], pair_in.at[d, l], pair_s.at[d, l], pair_r.at[d, l],
                 tok=partner,
             )
-    far = {}
+
+    def line_sum(d, l, primary):
+        upward = low_side if primary else jnp.logical_not(low_side)
+        way = jnp.where(upward, 0, 1)
+        target = mirror(d)
+        return pltpu.make_async_remote_copy(
+            src_ref=gram.at[target * 2 + core, l], dst_ref=line_in.at[way, target, l],
+            send_sem=gl_s.at[way, target, l], recv_sem=gl_r.at[way, target, l],
+            device_id={"tok": jnp.clip(jnp.where(upward, chip + 1, chip - 1), 0, chips - 1) * 2 + core},
+            device_id_type=pl.DeviceIdType.MESH,
+        )
+
+    def add_pair(d, l):
+        pair[d, l].wait_recv()
+        mine = mirror(d) * 2 + core
+        gram[mine, l] = gram[mine, l] + pair_in[d, l]
+
+    def arrive(d, l, primary):
+        upward = low_side if primary else jnp.logical_not(low_side)
+        way = jnp.where(upward, 0, 1)
+        target = mirror(d)
+        line_sum(d, l, primary).wait_recv()
+        mine = target * 2 + core
+        gram[mine, l] = gram[mine, l] + line_in[way, target, l]
+
+    def arrive_own(l, primary):
+        upward = low_side if primary else jnp.logical_not(low_side)
+        way = jnp.where(upward, 0, 1)
+        pltpu.make_async_remote_copy(
+            src_ref=gram.at[tok, l], dst_ref=line_in.at[way, chip, l],
+            send_sem=gl_s.at[way, chip, l], recv_sem=gl_r.at[way, chip, l],
+            device_id={"tok": partner}, device_id_type=pl.DeviceIdType.MESH,
+        ).wait_recv()
+        gram[tok, l] = gram[tok, l] + line_in[way, chip, l]
+
+    def forward(d, l, primary):
+        @pl.when(d > rank if primary else d < rank)
+        def _():
+            if primary:
+                @pl.when(rank > 0)
+                def _():
+                    arrive(d, l, primary)
+            else:
+                arrive(d, l, primary)
+            line_sum(d, l, primary).start()
+
+    def correct():
+        for copy in mean_copies:
+            copy.wait_recv()
+        overall = mean_out[...]
+        for k in range(1, groups):
+            overall = overall + means[k - 1]
+        overall = overall / groups
+        for l in range(layers):
+            shifts = [mean_out[l : l + 1] - overall[l : l + 1]]
+            for k in range(1, groups):
+                shifts.append(means[k - 1, l : l + 1] - overall[l : l + 1])
+            shifts = jnp.concatenate(shifts, axis=0)
+            outer = lax.dot_general(
+                shifts, shifts * tok_rows, (((0,), (0,)), ((), ())),
+                precision=lax.Precision.HIGHEST, preferred_element_type=F32,
+            )
+            for t in range(groups):
+                corr[t, l] = outer[t * slab : (t + 1) * slab]
+
+    steps = []
+    for d in range(chips):
+        for l in range(layers):
+            turn = (chips - 1 - d) * layers + l
+            steps.append((turn, 1, d, l))
+            if d < chips - 1:
+                steps.append((d * layers + l + layers - 0.5, 0, d, l))
+    early = True
+    for turn, primary, d, l in sorted(steps):
+        if turn > layers - 1 and early:
+            early = False
+            for other in outward[1:]:
+                for m in range(layers):
+                    add_pair(other, m)
+            correct()
+        if early:
+            add_pair(d, l)
+        if d > 0 or not primary:
+            forward(d, l, bool(primary))
+
+    edge = None
     for l in range(layers):
-        for k in list(range(1, chips)) + [0]:
-            other = flip(chip, k, chips) * 2 + core
-            pair[k, l].wait_recv()
-            gram[other, l] = gram[other, l] + pair_in[k, l]
-            if k:
-                far[k, l] = send(
-                    gram.at[other, l], line_in.at[k - 1, l], gl_s.at[k - 1, l], gl_r.at[k - 1, l],
-                    tok=other,
-                )
-
-    for copy in mean_copies:
-        copy.wait_recv()
-    overall = mean_out[...]
-    for k in range(1, groups):
-        overall = overall + means[k - 1]
-    overall = overall / groups
-    for l in range(layers):
-        shifts = [mean_out[l : l + 1] - overall[l : l + 1]]
-        for k in range(1, groups):
-            shifts.append(means[k - 1, l : l + 1] - overall[l : l + 1])
-        shifts = jnp.concatenate(shifts, axis=0)
-        outer = lax.dot_general(
-            shifts, shifts * tok_rows, (((0,), (0,)), ((), ())),
-            precision=lax.Precision.HIGHEST, preferred_element_type=F32,
-        )
-        for t in range(groups):
-            corr[t, l] = outer[t * slab : (t + 1) * slab]
-
-    edge = {}
-    for l in range(layers):
+        @pl.when(rank > 0)
+        def _():
+            arrive_own(l, True)
+
+        arrive_own(l, False)
         result = gram[tok, l] + corr[tok, l]
-        for k in range(1, chips):
-            far[k, l].wait_recv()
-            result = result + line_in[k - 1, l]
         sketch_ref[l] = result
         if l == 0:
-            edge_out[0] = result.astype(BF16)
-            edge[0] = send(
-                edge_out.at[0], edge_in.at[0], edge_s.at[0], edge_r.at[0],
-                section=(section + sections - 1) % sections,
-            )
-        if l == layers - 1:
-            edge_out[1] = result.astype(BF16)
-            edge[1] = send(
-                edge_out.at[1], edge_in.at[1], edge_s.at[1], edge_r.at[1],
-                section=(section + 1) % sections,
+            edge_out[...] = result.astype(BF16)
+            edge = send(
+                edge_out, edge_in, edge_s, edge_r, section=(section + sections - 1) % sections
             )
 
     def inner(first, second):
@@ -253,30 +342,43 @@
         if l:
             prod_out[layers + l - 1 : layers + l] = inner(own[l - 1], own[l])
     base = 2 * layers - 1
-    edge[0].wait_recv()
-    beyond = jnp.where(section == sections - 1, own[-1], edge_in[0].astype(F32))
+    edge.wait_recv()
+    beyond = edge_in[...].astype(F32)
     prod_out[base : base + 1] = inner(own[-1], beyond)
     prod_out[base + 1 : base + 2] = inner(beyond, beyond)
-    edge[1].wait_recv()
-    before = jnp.where(section == 0, own[0], edge_in[1].astype(F32))
-    prod_out[base + 2 : base + 3] = inner(own[0], before)
-    prod_out[base + 3 : base + 4] = inner(before, before)
-    prod_copies = []
-    for k in range(1, groups):
-        prod_copies.append(
-            send(prod_out, prods.at[k - 1], prod_s.at[k - 1], prod_r.at[k - 1], tok=flip(tok, k, groups))
-        )
+    prod_copies, prev_copies = [], []
+    for k in range(groups):
+        other = flip(tok, k, groups)
+        prev_copies.append(
+            send(prod_out, prev_prods.at[k], prev_s.at[k], prev_r.at[k],
+                 section=(section + 1) % sections, tok=other)
+        )
+        if k:
+            prod_copies.append(
+                send(prod_out, prods.at[k - 1], prod_s.at[k - 1], prod_r.at[k - 1], tok=other)
+            )
     products = prod_out[...]
     for k in range(1, groups):
         prod_copies[k - 1].wait_recv()
         products = products + prods[k - 1]
+    prev_copies[0].wait_recv()
+    earlier = prev_prods[0]
+    for k in range(1, groups):
+        prev_copies[k].wait_recv()
+        earlier = earlier + prev_prods[k]
     products = jnp.broadcast_to(jnp.sum(products, axis=1, keepdims=True), products.shape)
+    earlier = jnp.broadcast_to(jnp.sum(earlier, axis=1, keepdims=True), earlier.shape)
 
     def item(i):
         return products[i : i + 1]
 
-    squares = [item(base + 3)] + [item(l) for l in range(layers)] + [item(base + 1)]
-    chained = [item(base + 2)] + [item(layers + l) for l in range(layers - 1)] + [item(base)]
+    first, last = section == 0, section == sections - 1
+    before = jnp.where(first, item(0), earlier[layers - 1 : layers])
+    before_cross = jnp.where(first, item(0), earlier[base : base + 1])
+    beyond_square = jnp.where(last, item(layers - 1), item(base + 1))
+    beyond_cross = jnp.where(last, item(layers - 1), item(base))
+    squares = [before] + [item(l) for l in range(layers)] + [beyond_square]
+    chained = [before_cross] + [item(layers + l) for l in range(layers - 1)] + [beyond_cross]
     ratios = [chained[i] / jnp.sqrt(squares[i] * squares[i + 1]) for i in range(layers + 1)]
     sim_ref[...] = jnp.zeros_like(sim_ref)
     lane = lax.broadcasted_iota(jnp.int32, (1, 128), 1)
@@ -285,6 +387,15 @@
 
     for copy in pending:
         copy.wait_send()
+    for d in range(chips):
+        for l in range(layers):
+            for primary in (True, False):
+                @pl.when(d > rank if primary else d < rank)
+                def _():
+                    line_sum(d, l, primary).wait_send()
+    for source in [chip] + [t // 2 for t in order[2::2]]:
+        for h in range(2):
+            along(source, h, lambda copy: copy.wait_send())
 
 
 def local(sections, groups, activations, projection):
@@ -310,23 +421,25 @@
             pltpu.VMEM((layers, 3 * tok_rows, width), BF16),
             pltpu.VMEM((groups, layers, slab, width), F32),
             pltpu.VMEM((chips, layers, slab, width), F32),
-            pltpu.VMEM((chips - 1, layers, slab, width), F32),
+            pltpu.VMEM((2, chips, layers, slab, width), F32),
             pltpu.VMEM((tall, width), F32),
             pltpu.VMEM((groups - 1, tall, width), F32),
             pltpu.VMEM((groups, layers, slab, width), F32),
-            pltpu.VMEM((2, slab, width), BF16),
-            pltpu.VMEM((2, slab, width), BF16),
+            pltpu.VMEM((slab, width), BF16),
+            pltpu.VMEM((slab, width), BF16),
             pltpu.VMEM((tall, 128), F32),
             pltpu.VMEM((groups - 1, tall, 128), F32),
+            pltpu.VMEM((groups, tall, 128), F32),
             dma((groups,)), dma(()), dma((2,)),
-            dma((chips - 1, 2)), dma((chips - 1, 2)),
+            dma((chips, 2, 2)), dma((chips, 2)),
             dma((chips - 1, sections // 2, 2, 2)), dma((chips - 1, sections // 2, 2, 2)),
             dma((chips - 1, 2 * sections)), dma((chips - 1, 2 * sections)),
             dma((groups - 1,)), dma((groups - 1,)),
             dma((chips, layers)), dma((chips, layers)),
-            dma((chips - 1, layers)), dma((chips - 1, layers)),
-            dma((2,)), dma((2,)),
+            dma((2, chips, layers)), dma((2, chips, layers)),
+            dma(()), dma(()),
             dma((groups - 1,)), dma((groups - 1,)),
+            dma((groups,)), dma((groups,)),
         ],
         compiler_params=pltpu.CompilerParams(
             collective_id=0, has_side_effects=True, vmem_limit_bytes=60 * 1024 * 1024

time: 89.8 us -> 76.9 us (0.86)
  Pallas kernels: 86.1 us -> 73.1 us
    pallas_call x1, Pallas kernels: 86.1 us -> 73.1 us  [local(): pl.pallas_call(functools.partial(kernel, sections, groups, layers), out_s...]
where the time goes in v2:
time: 76.9 us; the launch traced here: 76.7 us
  Pallas kernels  73.1 us (95%)
  local copies, waits for them, and re-layouts  2.92 us (4%)
    pallas_call x1, Pallas kernels, local(): pl.pallas_call(functools.partial(kernel, sections, groups, layers), out_s...  73.1 us
    unnamed x1, local copies, waits for them, and re-layouts  1.67 us

profile of v2, /device:TPU:0, one launch (start us, length us, event | category | flops | bytes accessed | tf_op | source)
XLA Modules:
  0.0 76.7 jit_solution(18373178842432838613)
XLA Ops:
  0.6 73.1 %shard_map.41 = (f32[2,64,512]{2,1,0:T(8,128)}, f32[8,128]{1,0:T(8,128)}) custom-call(bf16[512,8192]{1,0:T(8,128)(2,1)} %bitcast.2, bf16[1024,512]{1,0:T(8,128)(2,1)} %proj_hbm.1), custom_call_target="tpu_custom_call" | custom-call | tf_op jit(solution)/shard_map/pallas_call | solution.py:408
  73.8 1.2 %slice.3 = f32[2,2]{1,0:T(2,128)} slice(f32[8,128]{1,0:T(8,128)} %get-tuple-element.5), slice={[0:2], [0:2]} | slice | bytes 32 | tf_op jit(solution)/shard_map/slice | solution.py:448
  75.0 1.7 %copy.5 = f32[2,512,64]{1,2,0:T(8,128)} copy(f32[2,512,64]{1,2,0:T(8,128)} %bitcast.3) | data formatting | bytes 524288

commit v3 on v2

--- a/solution.py
+++ b/solution.py
@@ -52,6 +52,7 @@
     half_ring = sections // 2
     piece = depth // sections
     part = piece // 2
+    cut = part // 2 if part % 32 == 0 else 0
     place = snake(section, sections)
     to_right = snake((place + 1) % sections, sections)
     to_left = snake((place + sections - 1) % sections, sections)
@@ -101,14 +102,23 @@
         pending.append(copy)
         return copy
 
-    def halves(t, at, h):
-        start = pl.multiple_of((at % sections) * piece + h * part, part)
-        return proj.at[t, pl.ds(start, part)]
+    def halves(t, at, h, last=False):
+        start, size = (at % sections) * piece + h * part, part
+        if last:
+            start, size = start + h * cut, part - cut
+        align = cut if cut else part
+        return proj.at[t, pl.ds(pl.multiple_of(start, align), size)]
+
+    def line_ref(t, h):
+        if h < 2:
+            return halves(t, place, h)
+        start = (place + half_ring) % sections * piece + part - cut
+        return proj.at[t, pl.ds(pl.multiple_of(start, cut), 2 * cut)]
 
     own_copy.wait()
 
     def line_copy(source, h, step):
-        ref = halves(source * 2 + core, place, h)
+        ref = line_ref(source * 2 + core, h)
         return pltpu.make_async_remote_copy(
             src_ref=ref, dst_ref=ref,
             send_sem=line_s.at[source, h, (step + 1) // 2], recv_sem=line_r.at[source, h],
@@ -127,6 +137,11 @@
 
     for h in range(2):
         along(chip, h, lambda copy: copy.start())
+    outer_chip = jnp.minimum(chip, chips - 1 - chip) == 0
+    if cut:
+        @pl.when(outer_chip)
+        def _():
+            along(chip, 2, lambda copy: copy.start())
     partner_slab = send(proj.at[tok], proj.at[tok], d2d_own.at[0], d2d_own.at[1], tok=partner)
 
     def multiply(n, first=False):
@@ -159,19 +174,29 @@
         events.append((0.75 * k + 0.2, k, 0))
         for j in range(1, half_ring + 1):
             events.append((1.5 * k + 1.4 * j - 1.1, k, j))
+        if cut:
+            events.append((0.75 * chips - 0.5 if k == 1 else 3.3 + 0.02 * k, k, -1))
         events.append((1.5 * k + 1.4 * half_ring - 0.9, k, half_ring + 1))
     for _, k, j in sorted(events):
         t = order[2 * k]
-        if j == 0:
+        source = t // 2
+        if j < 0:
+            line_copy(source, 2, 1).wait_recv()
+            along(source, 2, lambda copy: copy.start())
+            share(k, line_ref(t, 2))
+        elif j == 0:
             for h in range(2):
-                source = t // 2
                 line_copy(source, h, 1).wait_recv()
                 ref = halves(t, place, h)
                 along(source, h, lambda copy: copy.start())
                 for way in range(2):
                     if half_ring > 1 or way == h:
-                        pass_on(k, 1, way, h, ref)
+                        pass_on(k, 1, way, h, halves(t, place, h, half_ring == 1))
                 share(k, ref)
+            if k == min(2, chips - 1) and cut:
+                @pl.when(jnp.logical_not(outer_chip))
+                def _():
+                    along(chip, 2, lambda copy: copy.start())
         elif j <= half_ring:
             for h in range(2):
                 for way in range(2):
@@ -179,10 +204,9 @@
                         continue
                     ring[k, j, way, h].wait_recv()
                     at = place + sections - j if way == 0 else place + j
-                    ref = halves(t, at, h)
                     if j < half_ring and (j + 1 < half_ring or way == h):
-                        pass_on(k, j + 1, way, h, ref)
-                    share(k, ref)
+                        pass_on(k, j + 1, way, h, halves(t, at, h, j + 1 == half_ring))
+                    share(k, halves(t, at, h, j == half_ring))
         else:
             multiply(2 * k)
             for copy in shared[k]:
@@ -394,8 +418,13 @@
                 def _():
                     line_sum(d, l, primary).wait_send()
     for source in [chip] + [t // 2 for t in order[2::2]]:
-        for h in range(2):
+        for h in range(3 if cut else 2):
             along(source, h, lambda copy: copy.wait_send())
+
+
+def finish(sketch_in, sim_in, sketch_out, sim_out):
+    sketch_out[...] = sketch_in[...]
+    sim_out[...] = sim_in[: sim_out.shape[0], : sim_out.shape[1]]
 
 
 def local(sections, groups, activations, projection):
@@ -431,9 +460,9 @@
             pltpu.VMEM((groups - 1, tall, 128), F32),
             pltpu.VMEM((groups, tall, 128), F32),
             dma((groups,)), dma(()), dma((2,)),
-            dma((chips, 2, 2)), dma((chips, 2)),
+            dma((chips, 3, 2)), dma((chips, 3)),
             dma((chips - 1, sections // 2, 2, 2)), dma((chips - 1, sections // 2, 2, 2)),
-            dma((chips - 1, 2 * sections)), dma((chips - 1, 2 * sections)),
+            dma((chips - 1, 2 * sections + 1)), dma((chips - 1, 2 * sections + 1)),
             dma((groups - 1,)), dma((groups - 1,)),
             dma((chips, layers)), dma((chips, layers)),
             dma((2, chips, layers)), dma((2, chips, layers)),
@@ -445,7 +474,16 @@
             collective_id=0, has_side_effects=True, vmem_limit_bytes=60 * 1024 * 1024
         ),
     )(activations.reshape(rows, model_width), projection)
-    return jnp.swapaxes(sketch, 1, 2), sim[:layers, :2]
+    sketch, similarity = pl.pallas_call(
+        finish,
+        out_shape=(
+            jax.ShapeDtypeStruct((layers, slab, width), F32),
+            jax.ShapeDtypeStruct((layers, 2), F32),
+        ),
+        in_specs=[pl.BlockSpec(memory_space=pltpu.VMEM)] * 2,
+        out_specs=(pl.BlockSpec(memory_space=pltpu.VMEM),) * 2,
+    )(sketch, sim)
+    return jnp.swapaxes(sketch, 1, 2), similarity
 
 
 def solution(mesh):

time: 76.9 us -> 73.7 us (0.958)
  local copies, waits for them, and re-layouts: 2.92 us -> 0 us
    pallas_call x1, Pallas kernels: 73.1 us -> 71.2 us  [local(): pl.pallas_call(functools.partial(kernel, sections, groups, layers), out_s...]
    pallas_call x0 -> x1, Pallas kernels: none -> 1.68 us  [local(): pl.pallas_call(finish, out_shape=(jax.ShapeDtypeStruct((layers, slab, wid...]
    unnamed x1 -> x0, local copies, waits for them, and re-layouts: 1.67 us -> none
    slice x1 -> x0, local copies, waits for them, and re-layouts: 1.25 us -> none  [local(): return (jnp.swapaxes(sketch, 1, 2), sim[:layers, :2])]
where the time goes in v3:
time: 73.7 us; the launch traced here: 73.5 us
  Pallas kernels  72.9 us (99%)
    pallas_call x1, Pallas kernels, local(): pl.pallas_call(functools.partial(kernel, sections, groups, layers), out_s...  71.2 us
    pallas_call x1, Pallas kernels, local(): pl.pallas_call(finish, out_shape=(jax.ShapeDtypeStruct((layers, slab, wid...  1.68 us

profile of v3, /device:TPU:0, one launch (start us, length us, event | category | flops | bytes accessed | tf_op | source)
XLA Modules:
  0.0 73.5 jit_solution(4280880745004702719)
XLA Ops:
  0.6 71.2 %shard_map.41 = (f32[2,64,512]{2,1,0:T(8,128)}, f32[8,128]{1,0:T(8,128)}) custom-call(bf16[512,8192]{1,0:T(8,128)(2,1)} %bitcast.2, bf16[1024,512]{1,0:T(8,128)(2,1)} %proj_hbm.1), custom_call_target="tpu_custom_call" | custom-call | tf_op jit(solution)/shard_map/pallas_call | solution.py:437
  71.9 1.7 %shard_map.42 = (f32[2,64,512]{2,1,0:T(8,128)}, f32[2,2]{1,0:T(2,128)}) custom-call(f32[2,64,512]{2,1,0:T(8,128)} %get-tuple-element.6.sketch_in, f32[8,128]{1,0:T(8,128)} %get-tuple-element.7.sim_in), custom_call_target="tpu_custom_call" | custom-call | tf_op jit(solution)/shard_map/pallas_call | solution.py:477

commit v4 on v3

--- a/solution.py
+++ b/solution.py
@@ -156,12 +156,21 @@
     partner_slab.wait_recv()
     multiply(1)
 
+    def multiply_piece(n, at):
+        rows_of = pl.ds(pl.multiple_of(at % sections * piece, piece), piece)
+        total[...] += jnp.dot(
+            acts[n, :, rows_of], proj[order[n], rows_of], preferred_element_type=F32
+        )
+
+    split_last = piece % 128 == 0
     shared = {k: [] for k in range(1, chips)}
+    late = {k: [] for k in range(1, chips)}
     ring = {}
 
-    def share(k, ref):
-        n = len(shared[k])
-        shared[k].append(send(ref, ref, d2d_s.at[k - 1, n], d2d_r.at[k - 1, n], tok=partner))
+    def share(k, ref, opposite=False):
+        n = len(shared[k]) + len(late[k])
+        copy = send(ref, ref, d2d_s.at[k - 1, n], d2d_r.at[k - 1, n], tok=partner)
+        (late if opposite else shared)[k].append(copy)
 
     def pass_on(k, j, way, h, ref):
         ring[k, j, way, h] = send(
@@ -176,14 +185,18 @@
             events.append((1.5 * k + 1.4 * j - 1.1, k, j))
         if cut:
             events.append((0.75 * chips - 0.5 if k == 1 else 3.3 + 0.02 * k, k, -1))
-        events.append((1.5 * k + 1.4 * half_ring - 0.9, k, half_ring + 1))
+        if k == chips - 1 and split_last:
+            events.append((1.5 * k + 1.4 * half_ring - 1.15, k, half_ring + 1))
+            events.append((1.5 * k + 1.4 * half_ring - 0.9, k, half_ring + 2))
+        else:
+            events.append((1.5 * k + 1.4 * half_ring - 0.9, k, half_ring + 1))
     for _, k, j in sorted(events):
         t = order[2 * k]
         source = t // 2
         if j < 0:
             line_copy(source, 2, 1).wait_recv()
             along(source, 2, lambda copy: copy.start())
-            share(k, line_ref(t, 2))
+            share(k, line_ref(t, 2), True)
         elif j == 0:
             for h in range(2):
                 line_copy(source, h, 1).wait_recv()
@@ -206,10 +219,28 @@
                     at = place + sections - j if way == 0 else place + j
                     if j < half_ring and (j + 1 < half_ring or way == h):
                         pass_on(k, j + 1, way, h, halves(t, at, h, j + 1 == half_ring))
-                    share(k, halves(t, at, h, j == half_ring))
+                    share(k, halves(t, at, h, j == half_ring), j == half_ring)
+        elif k == chips - 1 and split_last:
+            if j == half_ring + 1:
+                near = [place]
+                for step in range(1, half_ring):
+                    near += [place + step, place + sections - step]
+                loads[2 * k].wait()
+                for at in near:
+                    multiply_piece(2 * k, at)
+                for copy in shared[k]:
+                    copy.wait_recv()
+                loads[2 * k + 1].wait()
+                for at in near:
+                    multiply_piece(2 * k + 1, at)
+            else:
+                multiply_piece(2 * k, place + half_ring)
+                for copy in late[k]:
+                    copy.wait_recv()
+                multiply_piece(2 * k + 1, place + half_ring)
         else:
             multiply(2 * k)
-            for copy in shared[k]:
+            for copy in shared[k] + late[k]:
                 copy.wait_recv()
             multiply(2 * k + 1)
 

time: 73.7 us -> 73.1 us (level)
  no operation moved by 1% of the time
where the time goes in v4:
time: 73.1 us; the launch traced here: 73 us
  Pallas kernels  72.4 us (99%)
    pallas_call x1, Pallas kernels, local(): pl.pallas_call(functools.partial(kernel, sections, groups, layers), out_s...  70.7 us
    pallas_call x1, Pallas kernels, local(): pl.pallas_call(finish, out_shape=(jax.ShapeDtypeStruct((layers, slab, wid...  1.68 us

profile of v4, /device:TPU:0, one launch (start us, length us, event | category | flops | bytes accessed | tf_op | source)
XLA Modules:
  0.0 73.0 jit_solution(6173668127092937656)
XLA Ops:
  0.6 70.7 %shard_map.41 = (f32[2,64,512]{2,1,0:T(8,128)}, f32[8,128]{1,0:T(8,128)}) custom-call(bf16[512,8192]{1,0:T(8,128)(2,1)} %bitcast.2, bf16[1024,512]{1,0:T(8,128)(2,1)} %proj_hbm.1), custom_call_target="tpu_custom_call" | custom-call | tf_op jit(solution)/shard_map/pallas_call | solution.py:468
  71.3 1.7 %shard_map.42 = (f32[2,64,512]{2,1,0:T(8,128)}, f32[2,2]{1,0:T(2,128)}) custom-call(f32[2,64,512]{2,1,0:T(8,128)} %get-tuple-element.6.sketch_in, f32[8,128]{1,0:T(8,128)} %get-tuple-element.7.sim_in), custom_call_target="tpu_custom_call" | custom-call | tf_op jit(solution)/shard_map/pallas_call | solution.py:508
